TPU v7x, 32 devices: a whole 2x2x4 slice. The times are simulated.
32 devices in a mesh: blk: 16 (over z, y, core), grp: 2 (over x).
Axes of the slice: x: 2, y: 2, z: 4, core: 2. Of those that a mesh axis runs over, the one named last changes fastest.
Arguments:
- layer_one: bfloat16 [1792, 1024], P(('blk', 'grp')), may hold values from -6 to 6
- layer_two: bfloat16 [1792, 1024], P(('blk', 'grp')), may hold values from -6 to 6
- spread: int32 [2], replicated, may hold values from 1024 to 4096
Outputs:
- profiles: float32 [2, 1792], P(None, ('blk', 'grp'))
- alignment: float32 [], replicated
All inputs are finite; a program needn't handle non-finite values.
Results may differ from a plain program's by a relative error of at most 0.0003.
Values may be sent and summed in bfloat16 or wider, within the bound.
A program may use at most 128 MiB of HBM per device.

v0:
```python
import jax
import jax.numpy as jnp
from jax import lax
from jax.sharding import PartitionSpec as P

D = 1024


def kernel_block(rows, sq_rows, cols, scale, offset):
    sq_cols = jnp.sum(cols.astype(jnp.float32) ** 2, axis=1)
    inner = lax.dot_general(
        rows, cols, (((1,), (1,)), ((), ())), preferred_element_type=jnp.float32
    )
    dist = sq_rows[:, None] + sq_cols[None, :] - 2.0 * inner
    return jnp.exp(-dist / (2.0 * scale)) - offset


def shards(layer_one, layer_two, spread):
    scales = spread.astype(jnp.float32)
    offsets = jnp.exp(-D / scales)
    stacked = jnp.stack([layer_one, layer_two])
    paired = lax.all_gather(stacked, "grp", axis=1, tiled=True)
    sq_pair = jnp.sum(paired.astype(jnp.float32) ** 2, axis=2)
    block = lax.all_gather(stacked, "blk", axis=1, tiled=True)
    first = kernel_block(paired[0], sq_pair[0], block[0], scales[0], offsets[0])
    second = kernel_block(paired[1], sq_pair[1], block[1], scales[1], offsets[1])
    first, second = (first, second)
    rows_acc = jnp.stack([jnp.sum(first, axis=1), jnp.sum(second, axis=1)])
    prods = jnp.stack([jnp.sum(first * second), jnp.sum(first * first), jnp.sum(second * second)])
    rows_acc, prods = (rows_acc, prods)
    own_rows = lax.psum_scatter(rows_acc, "grp", scatter_dimension=1, tiled=True)
    total = own_rows.shape[1] * lax.axis_size("blk") * lax.axis_size("grp")
    row_terms = jnp.stack(
        [
            jnp.sum(own_rows[0]),
            jnp.sum(own_rows[1]),
            jnp.sum(own_rows[0] * own_rows[1]),
            jnp.sum(own_rows[0] * own_rows[0]),
            jnp.sum(own_rows[1] * own_rows[1]),
        ]
    )
    prods = lax.psum(prods, ("blk", "grp"))
    row_terms = lax.psum(row_terms, ("blk", "grp"))
    sum_one, sum_two = (row_terms[0], row_terms[1])
    c_cross, c_one, c_two = (row_terms[2], row_terms[3], row_terms[4])
    h_cross = prods[0] - 2.0 * c_cross / total + sum_one * sum_two / (total * total)
    h_one = prods[1] - 2.0 * c_one / total + sum_one * sum_one / (total * total)
    h_two = prods[2] - 2.0 * c_two / total + sum_two * sum_two / (total * total)
    alignment = h_cross / jnp.sqrt(h_one * h_two)
    profiles = jnp.stack(
        [own_rows[0] / jnp.sqrt(c_one / total), own_rows[1] / jnp.sqrt(c_two / total)]
    )
    return (profiles, alignment)


def solution(mesh):
    return jax.shard_map(
        shards,
        mesh=mesh,
        in_specs=(P(("blk", "grp"), None), P(("blk", "grp"), None), P()),
        out_specs=(P(None, ("blk", "grp")), P()),
        check_vma=False,
    )
```

profile of v0, /device:TPU:0, one launch (start us, length us, event | category | flops | bytes accessed | tf_op | source)
XLA Modules:
  0.0 135.6 jit_solution(13423032327136159622)
XLA Ops:
  7.2 0.0 all-gather.2.cloned.1.call-start
  7.2 1.7 %pad_maximum_fusion = bf16[2,56,1024]{2,1,0:T(8,128)(2,1)} fusion(bf16[1,56,1024]{2,1,0:T(8,128)(2,1)} %bitcast.70, bf16[1,56,1024]{2,1,0:T(8,128)(2,1)} %bitcast.71), kind=kLoop, calls=%fused_computation.24 | loop fusion | flops 114688 | bytes 458752 | tf_op jit(solution)/shard_map/stack | solution.py:21
  8.9 0.0 all-gather.2.cloned.1.call-update
  8.9 0.7 convert_element_type.14
  9.6 0.6 fusion.16
  11.5 1.2 dynamic-slice
  13.4 0.7 divide_exponential_fusion
  14.0 0.6 fusion.17
  14.6 9.5 %all_gather.6 = bf16[2,112,1024]{2,1,0:T(8,128)(2,1)S(1)} all-gather(bf16[2,56,1024]{2,1,0:T(8,128)(2,1)} %pad_maximum_fusion), channel_id=1, replica_groups=mesh['blk'=16,'grp'=2] {'grp'}, dimensions={1}, use_global_device_ids=true | all-gather | bytes 688128 | tf_op jit(solution)/shard_map/all_gather | solution.py:22
  24.1 0.2 multiply_reduce_fusion.2
  24.3 36.4 %all-gather.2.cloned.1.call-done = bf16[2,896,1024]{2,1,0:T(8,128)(2,1)} async-done(((bf16[2,56,1024]{2,1,0:T(8,128)(2,1)}), bf16[2,896,1024]{2,1,0:T(8,128)(2,1)}) %all-gather.2.cloned.1.call-update) | async-done | bytes 3670032 | tf_op jit(solution)/shard_map/all_gather | solution.py:24
  60.7 0.0 copy-start
  60.7 3.0 %multiply_reduce_fusion.1 = (f32[896]{0:T(1024)S(1)}, f32[896]{0:T(1024)S(1)}) fusion(bf16[2,896,1024]{2,1,0:T(8,128)(2,1)} %all-gather.2.cloned.1.call-done), kind=kLoop, calls=%fused_computation.1 | loop fusion | flops 5503232 | bytes 3677184 | tf_op jit(solution)/shard_map/reduce_sum | solution.py:10
  63.7 0.2 copy-done
  63.8 1.4 %fusion.10 = f32[112,896]{1,0:T(8,128)S(1)} fusion(bf16[2,896,1024]{2,1,0:T(8,128)(2,1)S(1)} %copy-done, bf16[2,112,1024]{2,1,0:T(8,128)(2,1)S(1)} %all_gather.6, f32[]{:T(128)} %bitcast.12, f32[]{:T(128)} %bitcast.11, f32[896]{0:T(1024)S(1)} %get-tuple-element.3, f32[112]{0:T(128)S(1)} %get-tuple-element.18), kind=kOutput, calls=%fused_computation.14 | convolution fusion | flops 206123008 | bytes 2470408 | tf_op jit(solution)/shard_map/dot_general | solution.py:11
  65.2 2.1 %multiply_reduce_fusion.5 = (f32[]{:T(128)}, f32[]{:T(128)}, f32[112]{0:T(128)S(1)}, f32[]{:T(128)}, f32[112]{0:T(128)S(1)}) fusion(f32[112,896]{1,0:T(8,128)S(1)} %fusion.10, f32[]{:T(128)} %bitcast.6, f32[]{:T(128)} %bitcast.5, bf16[2,896,1024]{2,1,0:T(8,128)(2,1)S(1)} %copy-done, bf16[2,112,1024]{2,1,0:T(8,128)(2,1)S(1)} %all_gather.6, ...), kind=kOutput, calls=%fused_computation.21 | convolution fusion | flops 206925600 | bytes 2471316 | tf_op jit(solution)/shard_map/dot_general | solution.py:11
  67.4 4.9 %all-reduce = f32[2,112]{1,0:T(2,128)S(1)} all-reduce(f32[2,112]{1,0:T(2,128)S(1)} %pad_maximum_fusion.1), channel_id=2, replica_groups=mesh['blk'=16,'grp'=2] {'grp'}, use_global_device_ids=true, to_apply=%region_5.0.clone | all-reduce | flops 224 | bytes 1792
  72.3 0.1 constant_dynamic-slice_fusion
  72.4 0.7 multiply_reduce_fusion.6
  73.0 2.0 %pad_maximum_fusion.3 = f32[3]{0:T(128)S(1)} fusion(f32[1]{0:T(128)} %bitcast.23, f32[1]{0:T(128)} %bitcast.22, f32[1]{0:T(128)} %bitcast.21), kind=kLoop, calls=%fused_computation.27 | loop fusion | flops 6 | bytes 24 | tf_op jit(solution)/shard_map/stack | solution.py:29
  75.0 3.2 %stack.64 = f32[5]{0:T(128)S(1)} concatenate(f32[1]{0:T(128)} %bitcast.14, f32[1]{0:T(128)} %bitcast.15, f32[1]{0:T(128)} %bitcast.16, f32[1]{0:T(128)} %bitcast.17, f32[1]{0:T(128)} %bitcast.18), dimensions={0} | concatenate | bytes 40 | tf_op jit(solution)/shard_map/stack | solution.py:33
  78.2 39.4 %all-reduce.1 = (f32[5]{0:T(128)S(1)}, f32[3]{0:T(128)S(1)}) all-reduce(f32[5]{0:T(128)S(1)} %stack.64, f32[3]{0:T(128)S(1)} %pad_maximum_fusion.3), channel_id=1, replica_groups=mesh['blk'=16,'grp'=2] {'blk','grp'}, use_global_device_ids=true, to_apply=%region_11.0 | all-reduce | flops 8 | bytes 64 | tf_op jit(solution)/shard_map/psum | solution.py:43
  117.6 0.7 fusion.14
  127.1 0.6 pad_maximum_fusion.2
  (3 shorter events, 0.0 us)
Async XLA Ops:
  7.2 53.5 %all-gather.2.cloned.1.call-start = ((), (), s32[]{:S(2)}) async-start(), calls=%async_computation | async-start | bytes 3899392 | tf_op jit(solution)/shard_map/all_gather | solution.py:24
  60.7 3.1 %copy-start = (bf16[2,896,1024]{2,1,0:T(8,128)(2,1)S(1)}, bf16[2,896,1024]{2,1,0:T(8,128)(2,1)}, u32[]{:S(2)}) copy-start(bf16[2,896,1024]{2,1,0:T(8,128)(2,1)} %all-gather.2.cloned.1.call-done) | copy-start | bytes 11010052
Sparse Core Ops, SparseCore 0:
  10.3 50.3 all-gather.1
where the time goes:
time: 136 us
  blocking collectives  53.8 us (40%)
  waiting for transfers between devices  36.4 us (27%)
  between operations  26 us (19%)
  other arithmetic  9.38 us (7%)
  local copies, waits for them, and re-layouts  6.55 us (5%)
  matrix products  3.5 us (3%)
    psum x1, blocking collectives, shards(): row_terms = lax.psum(row_terms, ('blk', 'grp'))  39.4 us
    all_gather x1, waiting for transfers between devices, shards(): block = lax.all_gather(stacked, 'blk', axis=1, tiled=True)  36.4 us
    all_gather x1, blocking collectives, shards(): paired = lax.all_gather(stacked, 'grp', axis=1, tiled=True)  9.49 us
    unnamed x1, blocking collectives  4.91 us
    dot_general x2, matrix products, kernel_block(): lax.dot_general(rows, cols, (((1,), (1,)), ((), ())), preferred_element_t...  3.5 us
    another operation x1, local copies, waits for them, and re-layouts, shards(): jnp.stack([jnp.sum(own_rows[0]), jnp.sum(own_rows[1]), jnp.sum(own_rows[0...  3.22 us
    reduce_sum x1, other arithmetic, kernel_block(): sq_cols = jnp.sum(cols.astype(jnp.float32) ** 2, axis=1)  2.99 us
  transfers between devices with their start and end apart: 1, of which 1 were waited for; matrix products, arithmetic and copies ran while one was open for 3% of the time, Pallas kernels for 0%

commit v1 on v0

--- a/solution.py
+++ b/solution.py
@@ -40,7 +40,7 @@
         ]
     )
     prods = lax.psum(prods, ("blk", "grp"))
-    row_terms = lax.psum(row_terms, ("blk", "grp"))
+    row_terms = lax.psum(lax.psum(row_terms, "grp"), "blk")
     sum_one, sum_two = (row_terms[0], row_terms[1])
     c_cross, c_one, c_two = (row_terms[2], row_terms[3], row_terms[4])
     h_cross = prods[0] - 2.0 * c_cross / total + sum_one * sum_two / (total * total)

time: 136 us -> 170 us (1.25)
  blocking collectives: 53.8 us -> 85.6 us
    psum x1 -> x3, blocking collectives: 39.4 us -> 71.2 us  [the longest x1 36.9 us: shards(): prods = lax.psum(prods, ('blk', 'grp'))]
  transfers between devices with their start and end apart: 1 -> 1, of which waited for: 1 -> 1; matrix products, arithmetic and copies ran while one was open for 3% -> 2% of each run, Pallas kernels for 0% -> 0%
where the time goes in v1:
time: 170 us; the launch traced here: 168 us
  blocking collectives  85.6 us (50%)
  waiting for transfers between devices  36.4 us (21%)
  between operations  26.2 us (15%)
  other arithmetic  9.38 us (6%)
  local copies, waits for them, and re-layouts  7.19 us (4%)
  matrix products  3.5 us (2%)
    psum x1, blocking collectives, shards(): prods = lax.psum(prods, ('blk', 'grp'))  36.9 us
    all_gather x1, waiting for transfers between devices, shards(): block = lax.all_gather(stacked, 'blk', axis=1, tiled=True)  36.4 us
    psum x2, blocking collectives, shards(): row_terms = lax.psum(lax.psum(row_terms, 'grp'), 'blk')  34.4 us
    all_gather x1, blocking collectives, shards(): paired = lax.all_gather(stacked, 'grp', axis=1, tiled=True)  9.49 us
    unnamed x1, blocking collectives  4.91 us
    dot_general x2, matrix products, kernel_block(): lax.dot_general(rows, cols, (((1,), (1,)), ((), ())), preferred_element_t...  3.5 us
  transfers between devices with their start and end apart: 1, of which 1 were waited for; matrix products, arithmetic and copies ran while one was open for 2% of the time, Pallas kernels for 0%

profile of v1, /device:TPU:0, one launch (start us, length us, event | category | flops | bytes accessed | tf_op | source)
XLA Modules:
  0.0 168.4 jit_solution(14954826032016480330)
XLA Ops:
  7.2 1.7 pad_maximum_fusion
  8.9 0.7 convert_element_type.14
  9.6 0.6 fusion.16
  11.5 1.2 dynamic-slice
  13.4 0.7 divide_exponential_fusion
  14.0 0.6 fusion.17
  14.6 9.5 %all_gather.6 = bf16[2,112,1024]{2,1,0:T(8,128)(2,1)S(1)} all-gather(bf16[2,56,1024]{2,1,0:T(8,128)(2,1)} %pad_maximum_fusion), channel_id=1, replica_groups=mesh['blk'=16,'grp'=2] {'grp'}, dimensions={1}, use_global_device_ids=true | all-gather | bytes 688128 | tf_op jit(solution)/shard_map/all_gather | solution.py:22
  24.1 0.2 multiply_reduce_fusion.2
  24.3 36.4 %all-gather.2.cloned.1.call-done = bf16[2,896,1024]{2,1,0:T(8,128)(2,1)} async-done(((bf16[2,56,1024]{2,1,0:T(8,128)(2,1)}), bf16[2,896,1024]{2,1,0:T(8,128)(2,1)}) %all-gather.2.cloned.1.call-update) | async-done | bytes 3670032 | tf_op jit(solution)/shard_map/all_gather | solution.py:24
  60.7 3.0 %multiply_reduce_fusion.1 = (f32[896]{0:T(1024)S(1)}, f32[896]{0:T(1024)S(1)}) fusion(bf16[2,896,1024]{2,1,0:T(8,128)(2,1)} %all-gather.2.cloned.1.call-done), kind=kLoop, calls=%fused_computation.1 | loop fusion | flops 5503232 | bytes 3677184 | tf_op jit(solution)/shard_map/reduce_sum | solution.py:10
  63.7 0.2 copy-done
  63.8 1.4 fusion.10
  65.2 2.1 %multiply_reduce_fusion.5 = (f32[]{:T(128)}, f32[]{:T(128)}, f32[112]{0:T(128)S(1)}, f32[]{:T(128)}, f32[112]{0:T(128)S(1)}) fusion(f32[112,896]{1,0:T(8,128)S(1)} %fusion.10, f32[]{:T(128)} %bitcast.6, f32[]{:T(128)} %bitcast.5, bf16[2,896,1024]{2,1,0:T(8,128)(2,1)S(1)} %copy-done, bf16[2,112,1024]{2,1,0:T(8,128)(2,1)S(1)} %all_gather.6, ...), kind=kOutput, calls=%fused_computation.21 | convolution fusion | flops 206925600 | bytes 2471316 | tf_op jit(solution)/shard_map/dot_general | solution.py:11
  67.4 4.9 %all-reduce = f32[2,112]{1,0:T(2,128)S(1)} all-reduce(f32[2,112]{1,0:T(2,128)S(1)} %pad_maximum_fusion.1), channel_id=2, replica_groups=mesh['blk'=16,'grp'=2] {'grp'}, use_global_device_ids=true, to_apply=%region_5.0.clone | all-reduce | flops 224 | bytes 1792
  72.3 0.1 constant_dynamic-slice_fusion
  72.4 0.7 multiply_reduce_fusion.6
  73.0 3.2 %stack.64 = f32[5]{0:T(128)S(1)} concatenate(f32[1]{0:T(128)} %bitcast.14, f32[1]{0:T(128)} %bitcast.15, f32[1]{0:T(128)} %bitcast.16, f32[1]{0:T(128)} %bitcast.17, f32[1]{0:T(128)} %bitcast.18), dimensions={0} | concatenate | bytes 40 | tf_op jit(solution)/shard_map/stack | solution.py:33
  76.2 4.9 %psum.21 = f32[5]{0:T(128)S(1)} all-reduce(f32[5]{0:T(128)S(1)} %stack.64), channel_id=1, replica_groups=mesh['blk'=16,'grp'=2] {'grp'}, use_global_device_ids=true, to_apply=%region_11.0 | all-reduce | flops 5 | bytes 40 | tf_op jit(solution)/shard_map/psum | solution.py:43
  81.2 29.5 %psum.22 = f32[5]{0:T(128)S(1)} all-reduce(f32[5]{0:T(128)S(1)} %psum.21), channel_id=1, replica_groups=mesh['blk'=16,'grp'=2] {'blk'}, use_global_device_ids=true, to_apply=%region_12.0 | all-reduce | flops 5 | bytes 40 | tf_op jit(solution)/shard_map/psum | solution.py:43
  110.6 0.6 fusion.15
  116.9 2.0 %pad_maximum_fusion.3 = f32[3]{0:T(128)S(1)} fusion(f32[1]{0:T(128)} %bitcast.23, f32[1]{0:T(128)} %bitcast.22, f32[1]{0:T(128)} %bitcast.21), kind=kLoop, calls=%fused_computation.27 | loop fusion | flops 6 | bytes 24 | tf_op jit(solution)/shard_map/stack | solution.py:29
  119.5 36.9 %psum.23 = f32[3]{0:T(128)S(1)} all-reduce(f32[3]{0:T(128)S(1)} %pad_maximum_fusion.3), channel_id=1, replica_groups=mesh['blk'=16,'grp'=2] {'blk','grp'}, use_global_device_ids=true, to_apply=%region_16.0 | all-reduce | flops 3 | bytes 24 | tf_op jit(solution)/shard_map/psum | solution.py:42
  156.4 0.7 fusion.14
  159.8 0.6 pad_maximum_fusion.2
  (6 shorter events, 0.1 us)
Async XLA Ops:
  7.2 53.5 %all-gather.2.cloned.1.call-start = ((), (), s32[]{:S(2)}) async-start(), calls=%async_computation | async-start | bytes 3899392 | tf_op jit(solution)/shard_map/all_gather | solution.py:24
  60.7 3.1 %copy-start = (bf16[2,896,1024]{2,1,0:T(8,128)(2,1)S(1)}, bf16[2,896,1024]{2,1,0:T(8,128)(2,1)}, u32[]{:S(2)}) copy-start(bf16[2,896,1024]{2,1,0:T(8,128)(2,1)} %all-gather.2.cloned.1.call-done) | copy-start | bytes 11010052
Sparse Core Ops, SparseCore 0:
  10.3 50.3 all-gather.1
